TPU v7x, 32 devices: a whole 2x2x4 slice. The times are simulated.
32 devices in a mesh: site: 8 (over z, x), dom: 4 (over y, core).
Axes of the slice: x: 2, y: 2, z: 4, core: 2. Of those that a mesh axis runs over, the one named last changes fastest.
Arguments:
- top_partial: float32 [16, 61, 4, 8192], P(None, None, 'dom', 'site'), may hold values from 0.001 to 1
- bottom_partial: float32 [16, 61, 4, 8192], P(None, None, 'dom', 'site'), may hold values from 0.001 to 1
- left_vectors: float32 [256, 61, 61], P('dom'), may hold values from 0.05 to 1
- right_vectors: float32 [256, 61, 61], P('dom'), may hold values from 0.05 to 1
- decay_rates: float32 [256, 61], P('dom'), may hold values from 0.05 to 8
- state_weights: float32 [256, 61], P('dom'), may hold values from 0.002 to 0.05
- part_rates: float32 [256], P('dom'), may hold values from 0.3 to 3
- branch_lengths: float32 [1997], replicated, may hold values from 0.02 to 0.5
- pattern_weights: int32 [4, 8192], P('dom', 'site'), may hold values from 0 to 9
- block_partition: int32 [4, 64], P('dom', 'site'), may hold values from 0 to 255
- chosen_branches: int32 [16], replicated, may hold values from 0 to 1996, as said below
Outputs:
- site_loglik: float32 [16, 4, 8192], P(None, 'dom', 'site')
- part_derivs: float32 [2, 16, 256], P(None, None, 'dom')
- new_lengths: float32 [1997], replicated
Inputs may be any that keep to these rules, and one draw needn't show every extreme that they name: `chosen_branches`: distinct branch numbers.
All inputs are finite; a program needn't handle non-finite values.
Results may differ from a plain program's by a relative error of at most 0.0003.
Values sent between devices are 32-bit elements; how exact they have to be, the bound alone decides.
A program may use at most 64 MiB of HBM per device.

v0:
```python
import jax
import jax.numpy as jnp
from jax import lax
from jax.sharding import PartitionSpec as P

BLK = 128


def project(upper, lower, vec_left, vec_right, state_w):
    scaled = upper * jnp.transpose(state_w)[None, :, :, None]
    lefts = jnp.einsum("binl,nik->bknl", scaled, vec_left, precision=lax.Precision.HIGHEST)
    rights = jnp.einsum("nkj,bjnl->bknl", vec_right, lower, precision=lax.Precision.HIGHEST)
    return (lefts, rights)


def finish(lefts, rights, exponent, times, weight_f):
    joint = lefts * rights
    expo = jnp.transpose(exponent)[None, :, :, None]
    decayed = joint * jnp.exp(expo * times[:, None, None, None])
    like_zero = jnp.sum(decayed, axis=1)
    like_one = jnp.sum(decayed * expo, axis=1)
    like_two = jnp.sum(decayed * expo * expo, axis=1)
    first = like_one / like_zero
    second = like_two / like_zero - first * first
    loglik = weight_f[None] * jnp.log(like_zero)
    sums = jnp.stack(
        [jnp.sum(weight_f[None] * first, axis=-1), jnp.sum(weight_f[None] * second, axis=-1)]
    )
    return (loglik, sums)


def on_device(
    top_partial,
    bottom_partial,
    left_vectors,
    right_vectors,
    decay_rates,
    state_weights,
    part_rates,
    branch_lengths,
    pattern_weights,
    block_partition,
    chosen_branches,
):
    times = branch_lengths[chosen_branches]
    branches = top_partial.shape[0]
    states = top_partial.shape[1]
    sites_here = top_partial.shape[3]
    nblocks = sites_here // BLK
    upper = top_partial.reshape(branches, states, nblocks, BLK)
    lower = bottom_partial.reshape(branches, states, nblocks, BLK)
    blocks = block_partition[0]
    owned = left_vectors.shape[0]
    groups = lax.axis_size("dom")
    parts_all = owned * groups
    wanted = lax.all_gather(block_partition, "dom", axis=0, tiled=True)
    relative = wanted - lax.axis_index("dom") * owned
    inside = jnp.logical_and(relative >= 0, relative < owned).astype(jnp.float32)
    clipped = jnp.clip(relative, 0, owned - 1)
    send_left = left_vectors[clipped] * inside[:, :, None, None]
    send_right = right_vectors[clipped] * inside[:, :, None, None]
    send_decay = decay_rates[clipped] * inside[:, :, None]
    send_weight = state_weights[clipped] * inside[:, :, None]
    send_rate = part_rates[clipped] * inside
    received = (
        lax.all_to_all(send_left, "dom", split_axis=0, concat_axis=0, tiled=True),
        lax.all_to_all(send_right, "dom", split_axis=0, concat_axis=0, tiled=True),
        lax.all_to_all(send_decay, "dom", split_axis=0, concat_axis=0, tiled=True),
        lax.all_to_all(send_weight, "dom", split_axis=0, concat_axis=0, tiled=True),
        lax.all_to_all(send_rate, "dom", split_axis=0, concat_axis=0, tiled=True),
    )
    vec_left = jnp.sum(received[0], axis=0)
    vec_right = jnp.sum(received[1], axis=0)
    decay_b = jnp.sum(received[2], axis=0)
    weight_b = jnp.sum(received[3], axis=0)
    rate_b = jnp.sum(received[4], axis=0)
    exponent = -decay_b * rate_b[:, None]
    lefts, rights = project(upper, lower, vec_left, vec_right, weight_b)
    weight_f = pattern_weights[0].astype(jnp.float32).reshape(nblocks, BLK)
    loglik, sums = finish(lefts, rights, exponent, times, weight_f)
    onehot = (blocks[:, None] == jnp.arange(parts_all, dtype=jnp.int32)[None, :]).astype(
        jnp.float32
    )
    part_local = jnp.einsum("abn,np->abp", sums, onehot, precision=lax.Precision.HIGHEST)
    everything = lax.psum(part_local, ("site", "dom"))
    share = lax.dynamic_slice_in_dim(everything, lax.axis_index("dom") * owned, owned, 2)
    totals = jnp.sum(everything, axis=2)
    updated = times - totals[0] / totals[1]
    new_lengths = branch_lengths.at[chosen_branches].set(updated)
    return (loglik.reshape(branches, 1, sites_here), share, new_lengths)


def solution(mesh):
    return jax.shard_map(
        on_device,
        mesh=mesh,
        in_specs=(
            P(None, None, "dom", "site"),
            P(None, None, "dom", "site"),
            P("dom", None, None),
            P("dom", None, None),
            P("dom", None),
            P("dom", None),
            P("dom"),
            P(),
            P("dom", "site"),
            P("dom", "site"),
            P(),
        ),
        out_specs=(P(None, "dom", "site"), P(None, None, "dom"), P()),
        check_vma=False,
    )
```

profile of v0, /device:TPU:0, one launch (start us, length us, event | category | flops | bytes accessed | tf_op | source)
XLA Modules:
  0.0 121.8 jit_solution(4191838396032848199)
XLA Ops:
  0.6 0.0 copy-start
  0.6 0.8 copy.76
  1.5 6.2 %all-gather = s32[4,1,8]{2,1,0:T(1,128)S(1)} all-gather(s32[1,1,8]{2,1,0:T(1,128)} %bitcast.55), channel_id=1, replica_groups=mesh['site'=8,'dom'=4] {'dom'}, dimensions={0}, use_global_device_ids=true | all-gather | bytes 160 | tf_op jit(solution)/shard_map/all_gather | solution.py:56
  7.7 0.1 reshape.73
  7.8 1.4 %gather_fusion.4 = f32[32]{0:T(128)S(1)} fusion(f32[64]{0:T(128)} %param.17, s32[1024]{0:T(1024)S(1)} %pad_clamp_fusion.1), kind=kCustom, calls=%fused_computation.4 | custom fusion | bytes 384 | tf_op jit(solution)/shard_map/gather | solution.py:64
  9.2 0.1 reshape.104
  9.3 0.6 bitcast_select_fusion
  9.9 3.2 %all-to-all-start.4 = ((f32[4,1,8]{2,1,0:T(1,128)}), f32[4,1,8]{2,1,0:T(1,128)S(1)}, u32[]{:S(2)}, u32[]{:S(2)}) async-start(f32[4,1,8]{2,1,0:T(1,128)} %bitcast.14), calls=%async_computation.4 | async-start | bytes 4096 | tf_op jit(solution)/shard_map/all_to_all | solution.py:70
  13.1 1.3 %gather_fusion.3 = f32[32,61]{1,0:T(8,128)S(1)} fusion(f32[64,61]{1,0:T(8,128)} %param.15, s32[1024]{0:T(1024)S(1)} %pad_clamp_fusion.1), kind=kCustom, calls=%fused_computation.3 | custom fusion | bytes 15744 | tf_op jit(solution)/shard_map/gather | solution.py:62
  14.4 1.3 %gather_fusion.1 = f32[32,61]{1,0:T(8,128)S(1)} fusion(f32[64,61]{1,0:T(8,128)} %param.16, s32[1024]{0:T(1024)S(1)} %pad_clamp_fusion.1), kind=kCustom, calls=%fused_computation.1 | custom fusion | bytes 15744 | tf_op jit(solution)/shard_map/gather | solution.py:63
  15.8 0.1 bitcast_multiply_fusion.2
  15.8 0.7 reshape.156
  16.5 0.3 all-to-all-done.4
  16.8 3.2 %all-to-all-start.3 = ((f32[4,1,488]{2,1,0:T(1,128)}), f32[4,1,488]{2,1,0:T(1,128)S(1)}, u32[]{:S(2)}, u32[]{:S(2)}) async-start(f32[4,1,488]{2,1,0:T(1,128)} %reshape.156), calls=%async_computation.3 | async-start | bytes 16384 | tf_op jit(solution)/shard_map/all_to_all | solution.py:68
  20.1 0.7 reshape.158
  20.7 0.0 copy-done
  20.7 2.7 %gather_fusion.2 = f32[32,61,61]{2,0,1:T(8,128)S(1)} fusion(f32[64,61,61]{2,0,1:T(8,128)S(1)} %copy-done, s32[1024]{0:T(1024)S(1)} %pad_clamp_fusion.1), kind=kCustom, calls=%fused_computation.2 | custom fusion | bytes 952704 | tf_op jit(solution)/shard_map/gather | solution.py:61
  23.5 4.4 %gather_fusion = f32[32,61,61]{2,0,1:T(8,128)} fusion(f32[64,61,61]{2,0,1:T(8,128)} %param.13, s32[1024]{0:T(1024)S(1)} %pad_clamp_fusion.1), kind=kCustom, calls=%fused_computation | custom fusion | bytes 952704 | tf_op jit(solution)/shard_map/gather | solution.py:60
  27.9 0.0 all-to-all-done.3
  27.9 3.8 %all-to-all-start.1 = ((f32[4,1,488]{2,1,0:T(1,128)}), f32[4,1,488]{2,1,0:T(1,128)S(1)}, u32[]{:S(2)}, u32[]{:S(2)}) async-start(f32[4,1,488]{2,1,0:T(1,128)} %reshape.158), calls=%async_computation.1 | async-start | bytes 16384 | tf_op jit(solution)/shard_map/all_to_all | solution.py:69
  31.6 2.8 %copy_multiply_fusion.5 = (f32[4,8,61,61]{3,1,2,0:T(8,128)}, f32[4,8,61,61]{3,1,2,0:T(8,128)}) fusion(f32[4,8]{1,0:T(4,128)S(1)} %bitcast_convert_fusion, f32[32,61,61]{2,0,1:T(8,128)S(1)} %gather_fusion.2, f32[32,61,61]{2,0,1:T(8,128)} %gather_fusion), kind=kLoop, calls=%fused_computation.16 | loop fusion | flops 238144 | bytes 1905280 | tf_op jit(solution)/shard_map/mul | solution.py:60
  34.5 3.2 %reshape.160 = f32[4,1,29768]{2,1,0:T(1,128)} reshape(f32[4,61,8,61]{3,2,1,0:T(8,128)} %bitcast.46) | data formatting | bytes 952576
  37.6 0.0 all-to-all-done.1
  37.6 3.5 %all-to-all-start = ((f32[4,1,29768]{2,1,0:T(1,128)}), f32[4,1,29768]{2,1,0:T(1,128)S(1)}, u32[]{:S(2)}, u32[]{:S(2)}) async-start(f32[4,1,29768]{2,1,0:T(1,128)} %reshape.160), calls=%async_computation | async-start | bytes 954368 | tf_op jit(solution)/shard_map/all_to_all | solution.py:66
  41.1 0.0 copy-done.13
  41.1 0.0 copy-start.9
  41.1 3.1 %reshape.154 = f32[4,1,29768]{2,1,0:T(1,128)} reshape(f32[4,61,8,61]{3,2,1,0:T(8,128)} %bitcast.45) | data formatting | bytes 952576
  44.3 0.7 gather_fusion.5
  45.0 0.5 broadcast.86
  45.5 0.7 reduce.1
  46.2 0.1 reshape.157
  46.3 0.7 reduce.3
  47.0 0.1 reshape.159
  47.0 0.6 reduce_sum.100
  47.6 0.1 multiply_bitcast_fusion
  47.7 1.9 %all-to-all-done = f32[4,1,29768]{2,1,0:T(1,128)S(1)} async-done(((f32[4,1,29768]{2,1,0:T(1,128)}), f32[4,1,29768]{2,1,0:T(1,128)S(1)}, u32[]{:S(2)}, u32[]{:S(2)}) %all-to-all-start) | async-done | bytes 476320 | tf_op jit(solution)/shard_map/all_to_all | solution.py:66
  49.6 4.3 %all-to-all-start.2 = ((f32[4,1,29768]{2,1,0:T(1,128)}), f32[4,1,29768]{2,1,0:T(1,128)}, u32[]{:S(2)}, u32[]{:S(2)}) async-start(f32[4,1,29768]{2,1,0:T(1,128)} %reshape.154), calls=%async_computation.2 | async-start | bytes 954368 | tf_op jit(solution)/shard_map/all_to_all | solution.py:67
  53.9 0.1 multiply_exponential_fusion
  54.0 2.1 %reduce.4 = f32[4,29768]{1,0:T(4,128)S(1)} reduce(f32[4,1,29768]{2,1,0:T(1,128)S(1)} %all-to-all-done, f32[]{:T(128)} %broadcast.86), dimensions={1}, to_apply=%all_to_all.18.reduce_sub_computation | reduce | bytes 952580 | tf_op jit(solution)/shard_map/all_to_all | solution.py:66
  56.1 0.6 reshape.161
  56.7 0.8 bitcast_reduce_fusion
  57.4 4.7 %all-to-all-done.2 = f32[4,1,29768]{2,1,0:T(1,128)} async-done(((f32[4,1,29768]{2,1,0:T(1,128)}), f32[4,1,29768]{2,1,0:T(1,128)}, u32[]{:S(2)}, u32[]{:S(2)}) %all-to-all-start.2) | async-done | bytes 476320 | tf_op jit(solution)/shard_map/all_to_all | solution.py:67
  62.1 2.9 %reduce.2 = f32[4,29768]{1,0:T(4,128)S(1)} reduce(f32[4,1,29768]{2,1,0:T(1,128)} %all-to-all-done.2, f32[]{:T(128)} %broadcast.86), dimensions={1}, to_apply=%all_to_all.20.reduce_sub_computation | reduce | bytes 952580 | tf_op jit(solution)/shard_map/all_to_all | solution.py:67
  65.0 0.6 reshape.155
  65.6 0.1 bitcast_reduce_fusion.1
  65.7 0.0 copy-start.4
  65.7 0.0 copy-start.8
  65.7 0.0 copy-start.12
  65.7 6.8 %fusion = f32[8,61,16,128]{3,1,2,0:T(8,128)S(1)} fusion(f32[16,61,8,128]{3,2,1,0:T(8,128)} %bitcast.44, f32[8,61,61,1]{2,0,1,3:T(8,128)S(1)} %bitcast.47), kind=kOutput, calls=%fused_computation.8 | convolution fusion | flops 731578368 | bytes 8114464 | tf_op jit(solution)/shard_map/nkj,bjnl->bknl/dot_general | solution.py:12
  72.5 0.0 copy-done.2
  72.6 0.0 copy-done.4
  72.6 0.0 copy-done.8
  72.6 0.0 copy-done.12
  72.6 0.0 copy-start.11
  72.6 6.4 %multiply_reduce_fusion.1 = (f32[16,8,128]{2,0,1:T(8,128)S(1)}, f32[16,8,128]{2,0,1:T(8,128)S(1)}, f32[16,8,128]{2,0,1:T(8,128)S(1)}) fusion(f32[61,8]{0,1:T(8,128)S(1)} %copy-done.4, f32[16,61,8]{1,0,2:T(8,128)S(1)} %multiply_exponential_fusion, f32[8,61,16,128]{3,1,2,0:T(8,128)S(1)} %fusion, f32[16,61,8,128]{3,2,1,0:T(8,128)S(1)} %bitcast.57, ...), kind=kOutput, calls=%fused_computation.13 | convolution fusion | flops 739524608 | bytes 8346208 | tf_op jit(solution)/shard_map/binl,nik->bknl/dot_general | solution.py:11
  79.0 0.1 multiply_reduce_fusion.3
  79.2 0.2 fusion.6
  79.4 40.2 %psum.7 = f32[2,16,256]{2,1,0:T(8,128)S(1)} all-reduce(f32[2,16,256]{2,1,0:T(8,128)S(1)} %fusion.6), channel_id=1, replica_groups=mesh['site'=8,'dom'=4] {'site','dom'}, use_global_device_ids=true, to_apply=%region_10.11 | all-reduce | flops 8192 | bytes 65536 | tf_op jit(solution)/shard_map/psum | solution.py:85
  119.6 0.1 reduce_sum.109
  119.7 0.7 constant_dynamic-slice_fusion
  120.4 0.6 scatter_fusion
  121.1 0.0 copy-start.1
  121.1 0.7 copy.45
  121.8 0.0 copy-done.1
  (28 shorter events, 0.2 us)
Async XLA Ops:
  0.6 20.1 %copy-start = (f32[64,61,61]{2,0,1:T(8,128)S(1)}, f32[64,61,61]{2,0,1:T(8,128)}, u32[]{:S(2)}) copy-start(f32[64,61,61]{2,0,1:T(8,128)} %param.14) | copy-start | bytes 2857732
  9.9 6.9 %all-to-all-start.4 = ((f32[4,1,8]{2,1,0:T(1,128)}), f32[4,1,8]{2,1,0:T(1,128)S(1)}, u32[]{:S(2)}, u32[]{:S(2)}) async-start(f32[4,1,8]{2,1,0:T(1,128)} %bitcast.14), calls=%async_computation.4 | async-start | bytes 4096 | tf_op jit(solution)/shard_map/all_to_all | solution.py:70
  16.8 11.1 %all-to-all-start.3 = ((f32[4,1,488]{2,1,0:T(1,128)}), f32[4,1,488]{2,1,0:T(1,128)S(1)}, u32[]{:S(2)}, u32[]{:S(2)}) async-start(f32[4,1,488]{2,1,0:T(1,128)} %reshape.156), calls=%async_computation.3 | async-start | bytes 16384 | tf_op jit(solution)/shard_map/all_to_all | solution.py:68
  27.9 13.2 %copy-start.13 = (s32[16]{0:T(128)S(1)}, s32[16]{0:T(128)}, u32[]{:S(2)}) copy-start(s32[16]{0:T(128)} %param.21) | copy-start | bytes 196
  27.9 13.3 %copy-start.7 = (s32[1,1024]{1,0:T(1,128)S(1)}, s32[1,1024]{1,0:T(1,128)}, u32[]{:S(2)}) copy-start(s32[1,1024]{1,0:T(1,128)} %param.19) | copy-start | bytes 12292
  27.9 9.8 %all-to-all-start.1 = ((f32[4,1,488]{2,1,0:T(1,128)}), f32[4,1,488]{2,1,0:T(1,128)S(1)}, u32[]{:S(2)}, u32[]{:S(2)}) async-start(f32[4,1,488]{2,1,0:T(1,128)} %reshape.158), calls=%async_computation.1 | async-start | bytes 16384 | tf_op jit(solution)/shard_map/all_to_all | solution.py:69
  37.6 12.0 %all-to-all-start = ((f32[4,1,29768]{2,1,0:T(1,128)}), f32[4,1,29768]{2,1,0:T(1,128)S(1)}, u32[]{:S(2)}, u32[]{:S(2)}) async-start(f32[4,1,29768]{2,1,0:T(1,128)} %reshape.160), calls=%async_computation | async-start | bytes 954368 | tf_op jit(solution)/shard_map/all_to_all | solution.py:66
  41.1 3.2 %copy-start.9 = (s32[16]{0:T(128)}, s32[16]{0:T(128)S(1)}, u32[]{:S(2)}) copy-start(s32[16]{0:T(128)S(1)} %compare_select_fusion.1) | copy-start | bytes 196
  45.0 9.0 %copy-start.5 = (f32[16]{0:T(128)}, f32[16]{0:T(128)S(1)}, u32[]{:S(2)}) copy-start(f32[16]{0:T(128)S(1)} %gather_fusion.5) | copy-start | bytes 196
  47.7 6.3 %copy-start.3 = (f32[61,8]{0,1:T(8,128)}, f32[61,8]{0,1:T(8,128)S(1)}, u32[]{:S(2)}) copy-start(f32[61,8]{0,1:T(8,128)S(1)} %multiply_bitcast_fusion) | copy-start | bytes 5860
  49.6 12.5 %all-to-all-start.2 = ((f32[4,1,29768]{2,1,0:T(1,128)}), f32[4,1,29768]{2,1,0:T(1,128)}, u32[]{:S(2)}, u32[]{:S(2)}) async-start(f32[4,1,29768]{2,1,0:T(1,128)} %reshape.154), calls=%async_computation.2 | async-start | bytes 954368 | tf_op jit(solution)/shard_map/all_to_all | solution.py:67
  65.7 6.9 %copy-start.2 = (f32[8,61,61]{2,0,1:T(8,128)S(1)}, f32[8,61,61]{2,0,1:T(8,128)}, u32[]{:S(2)}) copy-start(f32[8,61,61]{2,0,1:T(8,128)} %bitcast_reduce_fusion) | copy-start | bytes 357220
  65.7 6.9 %copy-start.4 = (f32[61,8]{0,1:T(8,128)S(1)}, f32[61,8]{0,1:T(8,128)}, u32[]{:S(2)}) copy-start(f32[61,8]{0,1:T(8,128)} %copy-done.3) | copy-start | bytes 5860
  65.7 6.9 %copy-start.8 = (f32[8,61]{1,0:T(8,128)S(1)}, f32[8,61]{1,0:T(8,128)}, u32[]{:S(2)}) copy-start(f32[8,61]{1,0:T(8,128)} %reduce_sum.100) | copy-start | bytes 5860
  65.7 6.9 %copy-start.12 = (f32[16,61,1,1024]{3,2,1,0:T(1,128)S(1)}, f32[16,61,1,1024]{3,2,1,0:T(1,128)}, u32[]{:S(2)}) copy-start(f32[16,61,1,1024]{3,2,1,0:T(1,128)} %param.11) | copy-start | bytes 11993092
  72.6 6.6 %copy-start.11 = (s32[1,8]{1,0:T(1,128)S(1)}, s32[1,8]{1,0:T(1,128)}, u32[]{:S(2)}) copy-start(s32[1,8]{1,0:T(1,128)} %param.20) | copy-start | bytes 100
  72.6 47.8 %copy-start.6 = (f32[16]{0:T(128)S(1)}, f32[16]{0:T(128)}, u32[]{:S(2)}) copy-start(f32[16]{0:T(128)} %copy-done.5) | copy-start | bytes 196
  72.6 47.8 %copy-start.10 = (s32[16]{0:T(128)S(1)}, s32[16]{0:T(128)}, u32[]{:S(2)}) copy-start(s32[16]{0:T(128)} %copy-done.9) | copy-start | bytes 196
  121.1 0.8 copy-start.1
where the time goes:
time: 123 us; the launch traced here: 122 us
  blocking collectives  46.4 us (38%)
  local copies, waits for them, and re-layouts  24.4 us (20%)
  starting transfers between devices  18 us (15%)
  matrix products  13.5 us (11%)
  other arithmetic  11.7 us (10%)
  waiting for transfers between devices  6.84 us (6%)
    psum x1, blocking collectives, on_device(): everything = lax.psum(part_local, ('site', 'dom'))  40.2 us
    unnamed x38, local copies, waits for them, and re-layouts  10.6 us
    dot_general x1, matrix products, project(): jnp.einsum('nkj,bjnl->bknl', vec_right, lower, precision=lax.Precision.HI...  6.82 us
    dot_general x1, matrix products, project(): jnp.einsum('binl,nik->bknl', scaled, vec_left, precision=lax.Precision.HI...  6.42 us
    all_gather x1, blocking collectives, on_device(): wanted = lax.all_gather(block_partition, 'dom', axis=0, tiled=True)  6.22 us
    all_to_all x1, waiting for transfers between devices, on_device(): lax.all_to_all(send_right, 'dom', split_axis=0, concat_axis=0, tiled=True)  4.67 us
    gather x1, local copies, waits for them, and re-layouts, on_device(): send_left = left_vectors[clipped] * inside[:, :, None, None]  4.38 us
    all_to_all x1, starting transfers between devices, on_device(): lax.all_to_all(send_right, 'dom', split_axis=0, concat_axis=0, tiled=True)  4.3 us
  transfers between devices with their start and end apart: 5, of which 3 were waited for; matrix products, arithmetic and copies ran while one was open for 22% of the time, Pallas kernels for 0%

commit v1 on v0

v1 whole, which is shorter than its diff:
```python
import functools

import jax
import jax.numpy as jnp
from jax import lax
from jax.experimental import pallas as pl
from jax.experimental.pallas import tpu as pltpu
from jax.sharding import PartitionSpec as P

BLK = 128
MESH = pl.DeviceIdType.MESH
F32 = jnp.float32
BF16 = jnp.bfloat16


def round_up(value, unit):
    return (value + unit - 1) // unit * unit


def split(value):
    high = value.astype(BF16)
    return high, (value - high.astype(F32)).astype(BF16)


def body(
    cfg,
    top_hbm, bottom_hbm, left_hbm, right_hbm,
    decay_ref, weight_ref, rate_s, lengths_s, chosen_s, lengths_ref,
    pattern_ref, blocks_s, blocks_ref,
    loglik_ref, share_ref, new_ref,
    top_v, bottom_v, left_v, right_v, req_v, req_s, mine, passed, got,
    top_x, bottom_x, like_v, acc, dom_in, site_out, site_in,
    load_sem, req_send, req_recv, req_local, tab_send, tab_recv,
    dom_send, dom_recv, site_send, site_recv,
):
    doms, sites, branches, states, nblk, owned, pad, chunk = cfg
    me = lax.axis_index("dom")
    spot = lax.axis_index("site")
    dom_bits = doms.bit_length() - 1
    site_bits = sites.bit_length() - 1
    nchunk = nblk // chunk
    used = branches * states * nblk

    loads = [
        pltpu.make_async_copy(left_hbm, left_v, load_sem.at[0]),
        pltpu.make_async_copy(right_hbm, right_v, load_sem.at[1]),
        pltpu.make_async_copy(top_hbm, top_v.at[pl.ds(0, used)], load_sem.at[2]),
        pltpu.make_async_copy(bottom_hbm, bottom_v.at[pl.ds(0, used)], load_sem.at[3]),
    ]
    for load in loads:
        load.start()

    barrier = pltpu.get_barrier_semaphore()
    for delta in range(1, doms):
        pl.semaphore_signal(
            barrier, inc=1, device_id={"dom": me ^ delta}, device_id_type=MESH
        )
    for bit in range(site_bits):
        pl.semaphore_signal(
            barrier, inc=1, device_id={"site": spot ^ (1 << bit)}, device_id_type=MESH
        )

    req_v[0] = jnp.zeros((1, BLK), jnp.int32)
    req_v[0, 0:1, 0:nblk] = blocks_ref[...]
    tail = top_v.shape[0] - used
    top_v[pl.ds(used, tail), :] = jnp.zeros((tail, BLK), F32)
    bottom_v[pl.ds(used, tail), :] = jnp.zeros((tail, BLK), F32)
    mine[...] = jnp.zeros(mine.shape, F32)

    pl.semaphore_wait(barrier, doms - 1 + site_bits)

    asks = []
    for delta in range(1, doms):
        ask = pltpu.make_async_remote_copy(
            src_ref=req_v.at[0],
            dst_ref=req_v.at[delta],
            send_sem=req_send.at[delta],
            recv_sem=req_recv.at[delta],
            device_id={"dom": me ^ delta},
            device_id_type=MESH,
        )
        ask.start()
        asks.append(ask)
    loads[0].wait()
    loads[1].wait()
    for ask in asks:
        ask.wait()
    local = pltpu.make_async_copy(req_v, req_s, req_local)
    local.start()
    local.wait()

    def gather(delta):
        def step(n, carry):
            relative = req_s[delta, 0, n] - me * owned
            inside = jnp.logical_and(relative >= 0, relative < owned)
            keep = jnp.where(inside, 1.0, 0.0).astype(F32)
            p = jnp.clip(relative, 0, owned - 1)
            mine[delta, n, 0:states, 0:states] = left_v[p] * keep
            mine[delta, n, 0:states, pad:pad + states] = right_v[p] * keep
            rate = rate_s[p] * keep
            mine[delta, n, states:states + 1, pad:pad + states] = -decay_ref[pl.ds(p, 1), :] * rate
            mine[delta, n, states + 1:states + 2, pad:pad + states] = (
                weight_ref[pl.ds(p, 1), :] * keep
            )
            return carry

        lax.fori_loop(0, nblk, step, 0)

    def convert(n, carry):
        for source, dest in ((top_v, top_x), (bottom_v, bottom_x)):
            for b in range(branches):
                rows = source[pl.ds(b * states * nblk + n, pad, stride=nblk), :]
                high, low = split(rows)
                at = n * (branches // 2) + b // 2
                lanes = (b % 2) * BLK
                dest[at, 0:pad, lanes:lanes + BLK] = high
                dest[at, pad:2 * pad, lanes:lanes + BLK] = low
        return carry

    sends = {}
    for bit in range(dom_bits):
        moves = [d for d in range(doms) if d % (1 << bit) == 0 and (d >> bit) & 1]
        for d in sorted(moves, reverse=True):
            to = d ^ (1 << bit)
            for c in range(nchunk):
                at = pl.ds(c * chunk, chunk)
                sends[(bit, d, c)] = pltpu.make_async_remote_copy(
                    src_ref=(mine if bit == 0 else passed).at[d, at],
                    dst_ref=got.at[bit, to, at],
                    send_sem=tab_send.at[bit, d, c],
                    recv_sem=tab_recv.at[bit, to, c],
                    device_id={"dom": me ^ (1 << bit)},
                    device_id_type=MESH,
                )

    first = [d for d in range(doms) if d & 1]
    for d in sorted(first, reverse=True):
        gather(d)
        for c in range(nchunk):
            sends[(0, d, c)].start()
    for d in sorted((d for d in range(doms) if not d & 1), reverse=True):
        gather(d)
    loads[2].wait()
    loads[3].wait()
    lax.fori_loop(0, nblk // 2, convert, 0)
    for bit in range(1, dom_bits):
        moves = [d for d in range(doms) if d % (1 << bit) == 0 and (d >> bit) & 1]
        for d in sorted(moves, reverse=True):
            for c in range(nchunk):
                at = pl.ds(c * chunk, chunk)
                total = mine[d, at]
                for earlier in range(bit):
                    sends[(earlier, d | (1 << earlier), c)].wait_recv()
                    total = total + got[earlier, d, at]
                passed[d, at] = total
                sends[(bit, d, c)].start()
    lax.fori_loop(nblk // 2, nblk, convert, 0)

    acc[...] = jnp.zeros(acc.shape, F32)
    lane = lax.broadcasted_iota(jnp.int32, (2 * branches, BLK), 1)
    times = [lengths_s[chosen_s[b]] for b in range(branches)]

    def block(n, carry):
        tile = mine[0, n]
        for bit in range(dom_bits):
            tile = tile + got[bit, 0, n]
        turned = jnp.transpose(tile)
        w_row = tile[states + 1:states + 2, pad:2 * pad]
        l_high, l_low = split(turned[0:pad, :] * w_row)
        r_high, r_low = split(tile[:, pad:2 * pad])
        l_all = jnp.concatenate([l_high, l_high, l_low], axis=1)
        r_all = jnp.concatenate([r_high, r_high, r_low], axis=1)
        expo = jnp.broadcast_to(turned[pad:2 * pad, states:states + 1], (pad, BLK))
        for half in range(branches // 2):
            at = n * (branches // 2) + half
            t_x = top_x[at]
            b_x = bottom_x[at]
            lefts = jnp.dot(
                l_all, jnp.concatenate([t_x, t_x[0:pad]], axis=0), preferred_element_type=F32
            )
            rights = jnp.dot(
                r_all, jnp.concatenate([b_x, b_x[0:pad]], axis=0), preferred_element_type=F32
            )
            joint = lefts * rights
            for side in range(2):
                b = 2 * half + side
                decayed = joint[:, side * BLK:(side + 1) * BLK] * jnp.exp(expo * times[b])
                once = decayed * expo
                twice = once * expo
                like_v[0, b:b + 1, :] = jnp.sum(decayed, axis=0, keepdims=True)
                like_v[1, b:b + 1, :] = jnp.sum(once, axis=0, keepdims=True)
                like_v[2, b:b + 1, :] = jnp.sum(twice, axis=0, keepdims=True)
        like0 = like_v[0]
        first_d = like_v[1] / like0
        second_d = like_v[2] / like0 - first_d * first_d
        w_sites = pattern_ref[pl.ds(n, 1), :].astype(F32)
        loglik_ref[pl.ds(n, branches, stride=nblk), :] = w_sites * jnp.log(like0)
        both = jnp.concatenate([first_d, second_d], axis=0) * w_sites
        sums = jnp.sum(both, axis=1, keepdims=True)
        p = blocks_s[0, n]
        for d in range(doms):
            hit = jnp.logical_and(lane + d * owned == p, lane < owned)
            hit = jnp.logical_or(hit, lane == owned)
            acc[d] = acc[d] + jnp.where(hit, sums, 0.0)
        return carry

    for c in range(nchunk):
        for bit in range(dom_bits):
            sends[(bit, 1 << bit, c)].wait_recv()
        lax.fori_loop(c * chunk, (c + 1) * chunk, block, 0)

    scatter = []
    for delta in range(1, doms):
        copy = pltpu.make_async_remote_copy(
            src_ref=acc.at[me ^ delta],
            dst_ref=dom_in.at[me],
            send_sem=dom_send.at[delta],
            recv_sem=dom_recv.at[delta],
            device_id={"dom": me ^ delta},
            device_id_type=MESH,
        )
        copy.start()
        scatter.append(copy)
    dom_in[me] = acc[me]
    for copy in scatter:
        copy.wait_recv()
    total = dom_in[0]
    for d in range(1, doms):
        total = total + dom_in[d]
    pending = []
    for bit in range(site_bits):
        site_out[bit] = total
        copy = pltpu.make_async_remote_copy(
            src_ref=site_out.at[bit],
            dst_ref=site_in.at[bit],
            send_sem=site_send.at[bit],
            recv_sem=site_recv.at[bit],
            device_id={"site": spot ^ (1 << bit)},
            device_id_type=MESH,
        )
        copy.start()
        pending.append(copy)
        copy.wait_recv()
        total = total + site_in[bit]

    share_ref[...] = total[:, 0:owned]
    sums = total[:, owned:owned + 1]
    ratio = sums[0:branches] / sums[branches:2 * branches]
    new = lengths_ref[...]
    place = lax.broadcasted_iota(jnp.int32, new.shape, 1)
    for b in range(branches):
        value = times[b] - ratio[b:b + 1, :]
        new = jnp.where(place == chosen_s[b], value, new)
    new_ref[...] = new

    for copy in scatter + pending:
        copy.wait_send()
    for copy in sends.values():
        copy.wait_send()


def on_device(
    top_partial,
    bottom_partial,
    left_vectors,
    right_vectors,
    decay_rates,
    state_weights,
    part_rates,
    branch_lengths,
    pattern_weights,
    block_partition,
    chosen_branches,
):
    doms = lax.axis_size("dom")
    sites = lax.axis_size("site")
    branches, states, _, sites_here = top_partial.shape
    nblk = sites_here // BLK
    owned = left_vectors.shape[0]
    tree = branch_lengths.shape[0]
    pad = round_up(states + 2, 64)
    chunk = 2 if nblk % 2 == 0 else 1
    nchunk = nblk // chunk
    dom_bits = doms.bit_length() - 1
    site_bits = sites.bit_length() - 1
    used = branches * states * nblk
    room = used + (pad - states) * nblk
    cfg = (doms, sites, branches, states, nblk, owned, pad, chunk)
    hbm = pl.BlockSpec(memory_space=pl.ANY)
    vmem = pl.BlockSpec(memory_space=pltpu.VMEM)
    smem = pl.BlockSpec(memory_space=pltpu.SMEM)
    tile = (pad, 2 * pad)
    dma = pltpu.SemaphoreType.DMA
    loglik, share, new = pl.pallas_call(
        functools.partial(body, cfg),
        out_shape=(
            jax.ShapeDtypeStruct((branches * nblk, BLK), F32),
            jax.ShapeDtypeStruct((2 * branches, owned), F32),
            jax.ShapeDtypeStruct((1, tree), F32),
        ),
        in_specs=[hbm, hbm, hbm, hbm, vmem, vmem, smem, smem, smem, vmem, vmem, smem, vmem],
        out_specs=(vmem, vmem, vmem),
        scratch_shapes=[
            pltpu.VMEM((room, BLK), F32),
            pltpu.VMEM((room, BLK), F32),
            pltpu.VMEM((owned, states, states), F32),
            pltpu.VMEM((owned, states, states), F32),
            pltpu.VMEM((doms, 1, BLK), jnp.int32),
            pltpu.SMEM((doms, 1, BLK), jnp.int32),
            pltpu.VMEM((doms, nblk) + tile, F32),
            pltpu.VMEM((doms, nblk) + tile, F32),
            pltpu.VMEM((dom_bits, doms, nblk) + tile, F32),
            pltpu.VMEM((nblk * branches // 2, 2 * pad, 2 * BLK), BF16),
            pltpu.VMEM((nblk * branches // 2, 2 * pad, 2 * BLK), BF16),
            pltpu.VMEM((3, branches, BLK), F32),
            pltpu.VMEM((doms, 2 * branches, BLK), F32),
            pltpu.VMEM((doms, 2 * branches, BLK), F32),
            pltpu.VMEM((site_bits, 2 * branches, BLK), F32),
            pltpu.VMEM((site_bits, 2 * branches, BLK), F32),
            dma((4,)),
            dma((doms,)),
            dma((doms,)),
            dma,
            dma((dom_bits, doms, nchunk)),
            dma((dom_bits, doms, nchunk)),
            dma((doms,)),
            dma((doms,)),
            dma((site_bits,)),
            dma((site_bits,)),
        ],
        compiler_params=pltpu.CompilerParams(
            collective_id=0, has_side_effects=True, vmem_limit_bytes=56 * 1024 * 1024
        ),
    )(
        top_partial.reshape(used, BLK),
        bottom_partial.reshape(used, BLK),
        left_vectors,
        right_vectors,
        decay_rates,
        state_weights,
        part_rates,
        branch_lengths,
        chosen_branches,
        branch_lengths.reshape(1, tree),
        pattern_weights.reshape(nblk, BLK),
        block_partition,
        block_partition,
    )
    return (
        loglik.reshape(branches, 1, sites_here),
        share.reshape(2, branches, owned),
        new.reshape(tree),
    )


def solution(mesh):
    return jax.shard_map(
        on_device,
        mesh=mesh,
        in_specs=(
            P(None, None, "dom", "site"),
            P(None, None, "dom", "site"),
            P("dom", None, None),
            P("dom", None, None),
            P("dom", None),
            P("dom", None),
            P("dom"),
            P(),
            P("dom", "site"),
            P("dom", "site"),
            P(),
        ),
        out_specs=(P(None, "dom", "site"), P(None, None, "dom"), P()),
        check_vma=False,
    )
```

time: 123 us -> 46.6 us (0.38)
  blocking collectives: 46.4 us -> 0 us
  Pallas kernels: 0 us -> 34.8 us
  starting transfers between devices: 18 us -> 0 us
  local copies, waits for them, and re-layouts: 24.4 us -> 10.8 us
  matrix products: 13.5 us -> 0 us
  other arithmetic: 11.7 us -> 0 us
  waiting for transfers between devices: 6.84 us -> 0 us
    psum x1 -> x0, blocking collectives: 40.2 us -> none  [on_device(): everything = lax.psum(part_local, ('site', 'dom'))]
    pallas_call x0 -> x1, Pallas kernels: none -> 34.8 us  [on_device(): pl.pallas_call(functools.partial(body, cfg), out_shape=(jax.ShapeDtypeStr...]
    all_to_all x5 -> x0, starting transfers between devices: 18 us -> none  [the longest x1 4.3 us: on_device(): lax.all_to_all(send_right, 'dom', split_axis=0, concat_axis=0, tiled=True)]
    dot_general x3 -> x0, matrix products: 13.5 us -> none  [the longest x1 6.82 us: project(): jnp.einsum('nkj,bjnl->bknl', vec_right, lower, precision=lax.Precision.HI...]
    gather x7 -> x0, local copies, waits for them, and re-layouts: 11.9 us -> none  [the longest x1 4.38 us: on_device(): send_left = left_vectors[clipped] * inside[:, :, None, None]]
    all_to_all x5 -> x0, waiting for transfers between devices: 6.84 us -> none  [the longest x1 4.67 us: on_device(): lax.all_to_all(send_right, 'dom', split_axis=0, concat_axis=0, tiled=True)]
    all_to_all x4 -> x0, other arithmetic: 6.36 us -> none  [the longest x1 2.92 us: on_device(): lax.all_to_all(send_right, 'dom', split_axis=0, concat_axis=0, tiled=True)]
    all_gather x1 -> x0, blocking collectives: 6.22 us -> none  [on_device(): wanted = lax.all_gather(block_partition, 'dom', axis=0, tiled=True)]
  transfers between devices with their start and end apart: 5 -> 0, of which waited for: 3 -> 0; matrix products, arithmetic and copies ran while one was open for 22% -> 0% of each run, Pallas kernels for 0% -> 0%
where the time goes in v1:
time: 46.6 us; the launch traced here: 46.2 us
  Pallas kernels  34.8 us (75%)
  local copies, waits for them, and re-layouts  10.8 us (23%)
  between operations  0.65 us (1%)
    pallas_call x1, Pallas kernels, on_device(): pl.pallas_call(functools.partial(body, cfg), out_shape=(jax.ShapeDtypeStr...  34.8 us
    unnamed x7, local copies, waits for them, and re-layouts  10.8 us

profile of v1, /device:TPU:0, one launch (start us, length us, event | category | flops | bytes accessed | tf_op | source)
XLA Modules:
  0.0 46.2 jit_solution(218024671488013483)
XLA Ops:
  0.6 0.0 copy-start
  0.6 4.2 %copy.14.left_hbm = f32[64,61,61]{2,1,0:T(8,128)} copy(f32[64,61,61]{2,0,1:T(8,128)} %param.13) | data formatting | bytes 1905152 | tf_op args[2]
  4.8 0.0 copy-done
  4.8 2.5 %copy.15.right_hbm = f32[64,61,61]{2,1,0:T(8,128)} copy(f32[64,61,61]{2,0,1:T(8,128)S(1)} %copy-done) | data formatting | bytes 1905152 | tf_op args[3]
  7.3 34.8 %shard_map.130 = (f32[128,128]{1,0:T(8,128)}, f32[32,64]{1,0:T(8,128)}, f32[1,1997]{1,0:T(1,128)}) custom-call(f32[7808,128]{1,0:T(8,128)} %bitcast.7, f32[7808,128]{1,0:T(8,128)} %bitcast.8, f32[64,61,61]{2,1,0:T(8,128)} %copy.14.left_hbm, f32[64,61,61]{2,1,0:T(8,128)} %copy.15.right_hbm, f32[64,61]{1,0:T(8,128)} %decay_ref.1, f32[64,61]{1,0:T(8,128)} %weight_ref.1, ...), custom_call_target="tpu_custom_call" | custom-call | tf_op jit(solution)/shard_map/pallas_call | solution.py:294
  42.1 1.5 %copy.20 = f32[16,1,1024]{2,1,0:T(1,128)} copy(f32[16,1,1024]{2,1,0:T(1,128)} %bitcast.9) | data formatting | bytes 131072
  43.6 1.3 %copy.21 = f32[2,16,64]{2,1,0:T(8,128)} copy(f32[2,16,64]{2,1,0:T(8,128)} %bitcast.11) | data formatting | bytes 16384
  44.9 1.3 %copy.22 = f32[1997]{0:T(1024)} copy(f32[1997]{0:T(1024)} %bitcast.12) | data formatting | bytes 15976
Async XLA Ops:
  0.6 4.2 %copy-start = (f32[64,61,61]{2,0,1:T(8,128)S(1)}, f32[64,61,61]{2,0,1:T(8,128)}, u32[]{:S(2)}) copy-start(f32[64,61,61]{2,0,1:T(8,128)} %param.14) | copy-start | bytes 2857732

commit v2 on v1

--- a/solution.py
+++ b/solution.py
@@ -25,21 +25,30 @@
 def body(
     cfg,
     top_hbm, bottom_hbm, left_hbm, right_hbm,
-    decay_ref, weight_ref, rate_s, lengths_s, chosen_s, lengths_ref,
+    decay_ref, weight_ref, rate_s, lengths_s, chosen_s,
     pattern_ref, blocks_s, blocks_ref,
-    loglik_ref, share_ref, new_ref,
+    like_ref, final_ref,
     top_v, bottom_v, left_v, right_v, req_v, req_s, mine, passed, got,
     top_x, bottom_x, like_v, acc, dom_in, site_out, site_in,
     load_sem, req_send, req_recv, req_local, tab_send, tab_recv,
     dom_send, dom_recv, site_send, site_recv,
 ):
-    doms, sites, branches, states, nblk, owned, pad, chunk = cfg
+    doms, sites, inner, branches, states, nblk, owned, pad, chunk = cfg
     me = lax.axis_index("dom")
     spot = lax.axis_index("site")
     dom_bits = doms.bit_length() - 1
-    site_bits = sites.bit_length() - 1
+    outer = sites // inner
+    near, far = lax.rem(spot, inner), spot // inner
     nchunk = nblk // chunk
     used = branches * states * nblk
+
+    plane = [(d, x) for d in range(doms) for x in range(inner) if d or x]
+
+    def in_plane(d, x):
+        return {"dom": me ^ d, "site": far * inner + lax.rem(near + x, inner)}
+
+    def in_line(k):
+        return {"site": lax.rem(far + k, outer) * inner + near}
 
     loads = [
         pltpu.make_async_copy(left_hbm, left_v, load_sem.at[0]),
@@ -51,14 +60,10 @@
         load.start()
 
     barrier = pltpu.get_barrier_semaphore()
-    for delta in range(1, doms):
-        pl.semaphore_signal(
-            barrier, inc=1, device_id={"dom": me ^ delta}, device_id_type=MESH
-        )
-    for bit in range(site_bits):
-        pl.semaphore_signal(
-            barrier, inc=1, device_id={"site": spot ^ (1 << bit)}, device_id_type=MESH
-        )
+    for d, x in plane:
+        pl.semaphore_signal(barrier, inc=1, device_id=in_plane(d, x), device_id_type=MESH)
+    for k in range(1, outer):
+        pl.semaphore_signal(barrier, inc=1, device_id=in_line(k), device_id_type=MESH)
 
     req_v[0] = jnp.zeros((1, BLK), jnp.int32)
     req_v[0, 0:1, 0:nblk] = blocks_ref[...]
@@ -67,7 +72,7 @@
     bottom_v[pl.ds(used, tail), :] = jnp.zeros((tail, BLK), F32)
     mine[...] = jnp.zeros(mine.shape, F32)
 
-    pl.semaphore_wait(barrier, doms - 1 + site_bits)
+    pl.semaphore_wait(barrier, len(plane) + outer - 1)
 
     asks = []
     for delta in range(1, doms):
@@ -89,14 +94,14 @@
     local.start()
     local.wait()
 
-    def gather(delta):
+    def gather(delta, c=None):
         def step(n, carry):
             relative = req_s[delta, 0, n] - me * owned
             inside = jnp.logical_and(relative >= 0, relative < owned)
             keep = jnp.where(inside, 1.0, 0.0).astype(F32)
             p = jnp.clip(relative, 0, owned - 1)
-            mine[delta, n, 0:states, 0:states] = left_v[p] * keep
-            mine[delta, n, 0:states, pad:pad + states] = right_v[p] * keep
+            mine[delta, n, 0:states, 0:states] = left_v[pl.ds(p, states, stride=owned), :] * keep
+            mine[delta, n, 0:states, pad:pad + states] = right_v[pl.ds(p, states, stride=owned), :] * keep
             rate = rate_s[p] * keep
             mine[delta, n, states:states + 1, pad:pad + states] = -decay_ref[pl.ds(p, 1), :] * rate
             mine[delta, n, states + 1:states + 2, pad:pad + states] = (
@@ -104,7 +109,10 @@
             )
             return carry
 
-        lax.fori_loop(0, nblk, step, 0)
+        if c is None:
+            lax.fori_loop(0, nblk, step, 0)
+        else:
+            lax.fori_loop(c * chunk, (c + 1) * chunk, step, 0)
 
     def convert(n, carry):
         for source, dest in ((top_v, top_x), (bottom_v, bottom_x)):
@@ -133,28 +141,35 @@
                     device_id_type=MESH,
                 )
 
-    first = [d for d in range(doms) if d & 1]
-    for d in sorted(first, reverse=True):
-        gather(d)
+    def forward(bit, d):
         for c in range(nchunk):
-            sends[(0, d, c)].start()
-    for d in sorted((d for d in range(doms) if not d & 1), reverse=True):
-        gather(d)
+            at = pl.ds(c * chunk, chunk)
+            total = mine[d, at]
+            for earlier in range(bit):
+                sends[(earlier, d | (1 << earlier), c)].wait_recv()
+                total = total + got[earlier, d, at]
+            passed[d, at] = total
+            sends[(bit, d, c)].start()
+
+    for d in reversed(range(doms)):
+        if d & 1 and d > 1:
+            for c in range(nchunk):
+                gather(d, c)
+                sends[(0, d, c)].start()
+    for d in reversed(range(2, doms)):
+        if not d & 1:
+            gather(d)
+    for bit in range(1, dom_bits):
+        for d in reversed(range(doms)):
+            if d % (1 << bit) == 0 and (d >> bit) & 1:
+                forward(bit, d)
+    for c in range(nchunk):
+        gather(1, c)
+        sends[(0, 1, c)].start()
+    gather(0)
     loads[2].wait()
     loads[3].wait()
-    lax.fori_loop(0, nblk // 2, convert, 0)
-    for bit in range(1, dom_bits):
-        moves = [d for d in range(doms) if d % (1 << bit) == 0 and (d >> bit) & 1]
-        for d in sorted(moves, reverse=True):
-            for c in range(nchunk):
-                at = pl.ds(c * chunk, chunk)
-                total = mine[d, at]
-                for earlier in range(bit):
-                    sends[(earlier, d | (1 << earlier), c)].wait_recv()
-                    total = total + got[earlier, d, at]
-                passed[d, at] = total
-                sends[(bit, d, c)].start()
-    lax.fori_loop(nblk // 2, nblk, convert, 0)
+    lax.fori_loop(0, nblk, convert, 0)
 
     acc[...] = jnp.zeros(acc.shape, F32)
     lane = lax.broadcasted_iota(jnp.int32, (2 * branches, BLK), 1)
@@ -194,7 +209,7 @@
         first_d = like_v[1] / like0
         second_d = like_v[2] / like0 - first_d * first_d
         w_sites = pattern_ref[pl.ds(n, 1), :].astype(F32)
-        loglik_ref[pl.ds(n, branches, stride=nblk), :] = w_sites * jnp.log(like0)
+        like_ref[pl.ds(n, branches, stride=nblk), :] = like0
         both = jnp.concatenate([first_d, second_d], axis=0) * w_sites
         sums = jnp.sum(both, axis=1, keepdims=True)
         p = blocks_s[0, n]
@@ -210,53 +225,73 @@
         lax.fori_loop(c * chunk, (c + 1) * chunk, block, 0)
 
     scatter = []
-    for delta in range(1, doms):
+    for d, x in reversed(plane):
         copy = pltpu.make_async_remote_copy(
-            src_ref=acc.at[me ^ delta],
-            dst_ref=dom_in.at[me],
-            send_sem=dom_send.at[delta],
-            recv_sem=dom_recv.at[delta],
-            device_id={"dom": me ^ delta},
+            src_ref=acc.at[me ^ d],
+            dst_ref=dom_in.at[me * inner + near],
+            send_sem=dom_send.at[d * inner + x],
+            recv_sem=dom_recv.at[d * inner + x],
+            device_id=in_plane(d, x),
             device_id_type=MESH,
         )
         copy.start()
         scatter.append(copy)
-    dom_in[me] = acc[me]
+    dom_in[me * inner + near] = acc[me]
     for copy in scatter:
         copy.wait_recv()
     total = dom_in[0]
-    for d in range(1, doms):
+    for d in range(1, doms * inner):
         total = total + dom_in[d]
-    pending = []
-    for bit in range(site_bits):
-        site_out[bit] = total
+    site_out[...] = total
+    spread = []
+    for k in range(1, outer):
         copy = pltpu.make_async_remote_copy(
-            src_ref=site_out.at[bit],
-            dst_ref=site_in.at[bit],
-            send_sem=site_send.at[bit],
-            recv_sem=site_recv.at[bit],
-            device_id={"site": spot ^ (1 << bit)},
+            src_ref=site_out,
+            dst_ref=site_in.at[far],
+            send_sem=site_send.at[k],
+            recv_sem=site_recv.at[k],
+            device_id=in_line(k),
             device_id_type=MESH,
         )
         copy.start()
-        pending.append(copy)
+        spread.append(copy)
+    site_in[far] = total
+    for copy in spread:
         copy.wait_recv()
-        total = total + site_in[bit]
-
-    share_ref[...] = total[:, 0:owned]
+    total = site_in[0]
+    for z in range(1, outer):
+        total = total + site_in[z]
+
     sums = total[:, owned:owned + 1]
     ratio = sums[0:branches] / sums[branches:2 * branches]
+    row = lax.broadcasted_iota(jnp.int32, (branches, BLK), 0)
+    old = jnp.zeros((branches, BLK), F32)
+    for b in range(branches):
+        old = jnp.where(row == b, times[b], old)
+    final_ref[0:2 * branches, :] = total
+    final_ref[2 * branches:3 * branches, :] = old - ratio
+
+    for copy in scatter + spread:
+        copy.wait_send()
+    for copy in sends.values():
+        copy.wait_send()
+
+
+def write(
+    cfg, like_ref, final_ref, pattern_ref, chosen_s, lengths_ref, loglik_ref, share_ref, new_ref
+):
+    branches, nblk, owned = cfg
+    weights = pattern_ref[...].astype(F32)
+    for b in range(branches):
+        rows = pl.ds(b * nblk, nblk)
+        loglik_ref[rows, :] = weights * jnp.log(like_ref[rows, :])
+    share_ref[...] = final_ref[0:2 * branches, 0:owned]
     new = lengths_ref[...]
     place = lax.broadcasted_iota(jnp.int32, new.shape, 1)
     for b in range(branches):
-        value = times[b] - ratio[b:b + 1, :]
+        value = final_ref[2 * branches + b:2 * branches + b + 1, 0:1]
         new = jnp.where(place == chosen_s[b], value, new)
     new_ref[...] = new
-
-    for copy in scatter + pending:
-        copy.wait_send()
-    for copy in sends.values():
-        copy.wait_send()
 
 
 def on_device(
@@ -282,29 +317,30 @@
     chunk = 2 if nblk % 2 == 0 else 1
     nchunk = nblk // chunk
     dom_bits = doms.bit_length() - 1
-    site_bits = sites.bit_length() - 1
+    inner = 2 if sites % 2 == 0 else 1
+    outer = sites // inner
     used = branches * states * nblk
     room = used + (pad - states) * nblk
-    cfg = (doms, sites, branches, states, nblk, owned, pad, chunk)
+    cfg = (doms, sites, inner, branches, states, nblk, owned, pad, chunk)
     hbm = pl.BlockSpec(memory_space=pl.ANY)
     vmem = pl.BlockSpec(memory_space=pltpu.VMEM)
     smem = pl.BlockSpec(memory_space=pltpu.SMEM)
     tile = (pad, 2 * pad)
     dma = pltpu.SemaphoreType.DMA
-    loglik, share, new = pl.pallas_call(
+    pattern = pattern_weights.reshape(nblk, BLK)
+    like, final = pl.pallas_call(
         functools.partial(body, cfg),
         out_shape=(
             jax.ShapeDtypeStruct((branches * nblk, BLK), F32),
-            jax.ShapeDtypeStruct((2 * branches, owned), F32),
-            jax.ShapeDtypeStruct((1, tree), F32),
+            jax.ShapeDtypeStruct((3 * branches, BLK), F32),
         ),
-        in_specs=[hbm, hbm, hbm, hbm, vmem, vmem, smem, smem, smem, vmem, vmem, smem, vmem],
-        out_specs=(vmem, vmem, vmem),
+        in_specs=[hbm, hbm, hbm, hbm, vmem, vmem, smem, smem, smem, vmem, smem, vmem],
+        out_specs=(vmem, vmem),
         scratch_shapes=[
             pltpu.VMEM((room, BLK), F32),
             pltpu.VMEM((room, BLK), F32),
-            pltpu.VMEM((owned, states, states), F32),
-            pltpu.VMEM((owned, states, states), F32),
+            pltpu.VMEM((states * owned, states), F32),
+            pltpu.VMEM((states * owned, states), F32),
             pltpu.VMEM((doms, 1, BLK), jnp.int32),
             pltpu.SMEM((doms, 1, BLK), jnp.int32),
             pltpu.VMEM((doms, nblk) + tile, F32),
@@ -314,19 +350,19 @@
             pltpu.VMEM((nblk * branches // 2, 2 * pad, 2 * BLK), BF16),
             pltpu.VMEM((3, branches, BLK), F32),
             pltpu.VMEM((doms, 2 * branches, BLK), F32),
-            pltpu.VMEM((doms, 2 * branches, BLK), F32),
-            pltpu.VMEM((site_bits, 2 * branches, BLK), F32),
-            pltpu.VMEM((site_bits, 2 * branches, BLK), F32),
+            pltpu.VMEM((doms * inner, 2 * branches, BLK), F32),
+            pltpu.VMEM((2 * branches, BLK), F32),
+            pltpu.VMEM((outer, 2 * branches, BLK), F32),
             dma((4,)),
             dma((doms,)),
             dma((doms,)),
             dma,
             dma((dom_bits, doms, nchunk)),
             dma((dom_bits, doms, nchunk)),
-            dma((doms,)),
-            dma((doms,)),
-            dma((site_bits,)),
-            dma((site_bits,)),
+            dma((doms * inner,)),
+            dma((doms * inner,)),
+            dma((outer,)),
+            dma((outer,)),
         ],
         compiler_params=pltpu.CompilerParams(
             collective_id=0, has_side_effects=True, vmem_limit_bytes=56 * 1024 * 1024
@@ -334,18 +370,27 @@
     )(
         top_partial.reshape(used, BLK),
         bottom_partial.reshape(used, BLK),
-        left_vectors,
-        right_vectors,
+        jnp.swapaxes(left_vectors, 0, 1).reshape(states * owned, states),
+        jnp.swapaxes(right_vectors, 0, 1).reshape(states * owned, states),
         decay_rates,
         state_weights,
         part_rates,
         branch_lengths,
         chosen_branches,
-        branch_lengths.reshape(1, tree),
-        pattern_weights.reshape(nblk, BLK),
+        pattern,
         block_partition,
         block_partition,
     )
+    loglik, share, new = pl.pallas_call(
+        functools.partial(write, (branches, nblk, owned)),
+        out_shape=(
+            jax.ShapeDtypeStruct((branches * nblk, BLK), F32),
+            jax.ShapeDtypeStruct((2 * branches, owned), F32),
+            jax.ShapeDtypeStruct((1, tree), F32),
+        ),
+        in_specs=[vmem, vmem, vmem, smem, vmem],
+        out_specs=(vmem, vmem, vmem),
+    )(like, final, pattern, chosen_branches, branch_lengths.reshape(1, tree))
     return (
         loglik.reshape(branches, 1, sites_here),
         share.reshape(2, branches, owned),

time: 46.6 us -> 32.2 us (0.69)
  local copies, waits for them, and re-layouts: 10.8 us -> 0 us
  Pallas kernels: 34.8 us -> 31.3 us
    unnamed x7 -> x0, local copies, waits for them, and re-layouts: 10.8 us -> none
    pallas_call x1, Pallas kernels: 34.8 us -> 29.6 us  [on_device(): pl.pallas_call(functools.partial(body, cfg), out_shape=(jax.ShapeDtypeStr...]
    pallas_call x0 -> x1, Pallas kernels: none -> 1.7 us  [on_device(): pl.pallas_call(functools.partial(write, (branches, nblk, owned)), out_sha...]
where the time goes in v2:
time: 32.2 us; the launch traced here: 32 us
  Pallas kernels  31.3 us (97%)
  between operations  0.64 us (2%)
    pallas_call x1, Pallas kernels, on_device(): pl.pallas_call(functools.partial(body, cfg), out_shape=(jax.ShapeDtypeStr...  29.6 us
    pallas_call x1, Pallas kernels, on_device(): pl.pallas_call(functools.partial(write, (branches, nblk, owned)), out_sha...  1.7 us

profile of v2, /device:TPU:0, one launch (start us, length us, event | category | flops | bytes accessed | tf_op | source)
XLA Modules:
  0.0 32.0 jit_solution(7197500811114017116)
XLA Ops:
  0.6 29.6 %shard_map.130 = (f32[128,128]{1,0:T(8,128)}, f32[48,128]{1,0:T(8,128)}) custom-call(f32[7808,128]{1,0:T(8,128)} %bitcast.13, f32[7808,128]{1,0:T(8,128)} %bitcast.14, f32[3904,61]{1,0:T(8,128)} %bitcast.15, f32[3904,61]{1,0:T(8,128)} %bitcast.16, f32[64,61]{1,0:T(8,128)} %decay_ref.1, f32[64,61]{1,0:T(8,128)} %weight_ref.1, f32[64]{0:T(128)} %rate_s.1, ...), custom_call_target="tpu_custom_call" | custom-call | tf_op jit(solution)/shard_map/pallas_call | solution.py:331
  30.3 1.7 %shard_map.131 = (f32[128,128]{1,0:T(8,128)}, f32[32,64]{1,0:T(8,128)}, f32[1,1997]{1,0:T(1,128)}) custom-call(f32[128,128]{1,0:T(8,128)} %get-tuple-element.8.like_ref, f32[48,128]{1,0:T(8,128)} %get-tuple-element.9.final_ref, s32[8,128]{1,0:T(8,128)} %bitcast.19, s32[16]{0:T(128)} %chosen_s.3, f32[1,1997]{1,0:T(1,128)} %bitcast.17), custom_call_target="tpu_custom_call" | custom-call | tf_op jit(solution)/shard_map/pallas_call | solution.py:384

commit v3 on v2

--- a/solution.py
+++ b/solution.py
@@ -25,12 +25,13 @@
 def body(
     cfg,
     top_hbm, bottom_hbm, left_hbm, right_hbm,
-    decay_ref, weight_ref, rate_s, lengths_s, chosen_s,
-    pattern_ref, blocks_s, blocks_ref,
+    decay_hbm, weight_hbm, rate_hbm, lengths_hbm, chosen_hbm,
+    pattern_hbm, blocks_hbm,
     like_ref, final_ref,
     top_v, bottom_v, left_v, right_v, req_v, req_s, mine, passed, got,
     top_x, bottom_x, like_v, acc, dom_in, site_out, site_in,
-    load_sem, req_send, req_recv, req_local, tab_send, tab_recv,
+    decay_ref, weight_ref, rate_s, lengths_s, chosen_s, pattern_ref, blocks_s, blocks_ref,
+    load_sem, small_sem, req_send, req_recv, req_local, tab_send, tab_recv,
     dom_send, dom_recv, site_send, site_recv,
 ):
     doms, sites, inner, branches, states, nblk, owned, pad, chunk = cfg
@@ -56,8 +57,19 @@
         pltpu.make_async_copy(top_hbm, top_v.at[pl.ds(0, used)], load_sem.at[2]),
         pltpu.make_async_copy(bottom_hbm, bottom_v.at[pl.ds(0, used)], load_sem.at[3]),
     ]
-    for load in loads:
-        load.start()
+    small = [
+        pltpu.make_async_copy(source, dest, small_sem.at[i])
+        for i, (source, dest) in enumerate((
+            (blocks_hbm, blocks_ref),
+            (decay_hbm, decay_ref),
+            (weight_hbm, weight_ref),
+            (rate_hbm, rate_s),
+            (blocks_hbm, blocks_s),
+            (lengths_hbm, lengths_s),
+            (chosen_hbm, chosen_s),
+            (pattern_hbm, pattern_ref),
+        ))
+    ]
 
     barrier = pltpu.get_barrier_semaphore()
     for d, x in plane:
@@ -65,13 +77,16 @@
     for k in range(1, outer):
         pl.semaphore_signal(barrier, inc=1, device_id=in_line(k), device_id_type=MESH)
 
+    for load in small + loads[:2]:
+        load.start()
     req_v[0] = jnp.zeros((1, BLK), jnp.int32)
-    req_v[0, 0:1, 0:nblk] = blocks_ref[...]
     tail = top_v.shape[0] - used
     top_v[pl.ds(used, tail), :] = jnp.zeros((tail, BLK), F32)
     bottom_v[pl.ds(used, tail), :] = jnp.zeros((tail, BLK), F32)
     mine[...] = jnp.zeros(mine.shape, F32)
 
+    small[0].wait()
+    req_v[0, 0:1, 0:nblk] = blocks_ref[...]
     pl.semaphore_wait(barrier, len(plane) + outer - 1)
 
     asks = []
@@ -86,8 +101,10 @@
         )
         ask.start()
         asks.append(ask)
-    loads[0].wait()
-    loads[1].wait()
+    for load in small[1:] + loads[:2]:
+        load.wait()
+    loads[2].start()
+    loads[3].start()
     for ask in asks:
         ask.wait()
     local = pltpu.make_async_copy(req_v, req_s, req_local)
@@ -112,7 +129,7 @@
         if c is None:
             lax.fori_loop(0, nblk, step, 0)
         else:
-            lax.fori_loop(c * chunk, (c + 1) * chunk, step, 0)
+            lax.fori_loop(c * chunk, (c + 1) * chunk, step, 0, unroll=True)
 
     def convert(n, carry):
         for source, dest in ((top_v, top_x), (bottom_v, bottom_x)):
@@ -222,7 +239,7 @@
     for c in range(nchunk):
         for bit in range(dom_bits):
             sends[(bit, 1 << bit, c)].wait_recv()
-        lax.fori_loop(c * chunk, (c + 1) * chunk, block, 0)
+        lax.fori_loop(c * chunk, (c + 1) * chunk, block, 0, unroll=True)
 
     scatter = []
     for d, x in reversed(plane):
@@ -334,7 +351,7 @@
             jax.ShapeDtypeStruct((branches * nblk, BLK), F32),
             jax.ShapeDtypeStruct((3 * branches, BLK), F32),
         ),
-        in_specs=[hbm, hbm, hbm, hbm, vmem, vmem, smem, smem, smem, vmem, smem, vmem],
+        in_specs=[hbm] * 11,
         out_specs=(vmem, vmem),
         scratch_shapes=[
             pltpu.VMEM((room, BLK), F32),
@@ -353,7 +370,16 @@
             pltpu.VMEM((doms * inner, 2 * branches, BLK), F32),
             pltpu.VMEM((2 * branches, BLK), F32),
             pltpu.VMEM((outer, 2 * branches, BLK), F32),
+            pltpu.VMEM((owned, states), F32),
+            pltpu.VMEM((owned, states), F32),
+            pltpu.SMEM((owned,), F32),
+            pltpu.SMEM((tree,), F32),
+            pltpu.SMEM((branches,), jnp.int32),
+            pltpu.VMEM((nblk, BLK), jnp.int32),
+            pltpu.SMEM((1, nblk), jnp.int32),
+            pltpu.VMEM((1, nblk), jnp.int32),
             dma((4,)),
+            dma((8,)),
             dma((doms,)),
             dma((doms,)),
             dma,
@@ -379,7 +405,6 @@
         chosen_branches,
         pattern,
         block_partition,
-        block_partition,
     )
     loglik, share, new = pl.pallas_call(
         functools.partial(write, (branches, nblk, owned)),

time: 32.2 us -> 29.6 us (0.919)
  Pallas kernels: 31.3 us -> 28.8 us
    pallas_call x1, Pallas kernels: 29.6 us -> 27.1 us  [on_device(): pl.pallas_call(functools.partial(body, cfg), out_shape=(jax.ShapeDtypeStr...]
where the time goes in v3:
time: 29.6 us; the launch traced here: 29.5 us
  Pallas kernels  28.8 us (97%)
  between operations  0.64 us (2%)
    pallas_call x1, Pallas kernels, on_device(): pl.pallas_call(functools.partial(body, cfg), out_shape=(jax.ShapeDtypeStr...  27.1 us
    pallas_call x1, Pallas kernels, on_device(): pl.pallas_call(functools.partial(write, (branches, nblk, owned)), out_sha...  1.7 us

profile of v3, /device:TPU:0, one launch (start us, length us, event | category | flops | bytes accessed | tf_op | source)
XLA Modules:
  0.0 29.5 jit_solution(3768964509149300711)
XLA Ops:
  0.6 27.1 %shard_map.130 = (f32[128,128]{1,0:T(8,128)}, f32[48,128]{1,0:T(8,128)}) custom-call(f32[7808,128]{1,0:T(8,128)} %bitcast.13, f32[7808,128]{1,0:T(8,128)} %bitcast.14, f32[3904,61]{1,0:T(8,128)} %bitcast.15, f32[3904,61]{1,0:T(8,128)} %bitcast.16, f32[64,61]{1,0:T(8,128)} %decay_hbm.1, f32[64,61]{1,0:T(8,128)} %weight_hbm.1, f32[64]{0:T(128)} %rate_hbm.1, ...), custom_call_target="tpu_custom_call" | custom-call | tf_op jit(solution)/shard_map/pallas_call | solution.py:348
  27.8 1.7 %shard_map.131 = (f32[128,128]{1,0:T(8,128)}, f32[32,64]{1,0:T(8,128)}, f32[1,1997]{1,0:T(1,128)}) custom-call(f32[128,128]{1,0:T(8,128)} %get-tuple-element.8.like_ref, f32[48,128]{1,0:T(8,128)} %get-tuple-element.9.final_ref, s32[8,128]{1,0:T(8,128)} %bitcast.19, s32[16]{0:T(128)} %chosen_s.1, f32[1,1997]{1,0:T(1,128)} %bitcast.17), custom_call_target="tpu_custom_call" | custom-call | tf_op jit(solution)/shard_map/pallas_call | solution.py:409
